TPU v7x, 32 devices: a whole 2x2x4 slice. The times are simulated.
32 devices in a mesh: section: 2 (over y), freq: 16 (over z, x, core).
Axes of the slice: x: 2, y: 2, z: 4, core: 2. Of those that a mesh axis runs over, the one named last changes fastest.
Arguments:
- spectra: float32 [4, 16, 131072], P('section', None, 'freq'), may hold values from 0.1 to 90, as said below
- channel_gain: float32 [131072], P('freq'), may hold values from 0.5 to 2
- bandpass_bin: int32 [131072], P('freq'), may hold values from 0 to 63, never falling along the last dimension, each value on 1 to 8192 neighbouring positions
- drift_range: int32 [4], replicated, may hold values from 1 to 2, as said below
- hit_cutoff: int32 [4, 2, 16], replicated, may hold values from 0 to 1023
Outputs:
- drift_score: float32 [4, 2, 131072], P(None, 'section', 'freq')
Inputs may be any that keep to these rules, and one draw needn't show every extreme that they name: `spectra`: every entry is positive. `bandpass_bin`: the bins never fall along the channels and each of the 64 bins holds 1 to 8192 channels. `drift_range`: some group reaches 2 and some other group searches stride 1 only.
All inputs are finite; a program needn't handle non-finite values.
Results may differ from a plain program's by a relative error of at most 0.0003.
Values sent between devices are 32-bit elements; how exact they have to be, the bound alone decides.
No kernel may reach another device: no remote copies, remote signals or barrier semaphores. Data moves between devices by JAX's collectives and lax.ppermute only.
A program may use at most 64 MiB of HBM per device.

v0:
```python
import jax
import jax.numpy as jnp
from jax import lax
from jax.sharding import PartitionSpec as P


def carried_in(value, axis, join, neutral):
    count, mine = (lax.axis_size(axis), lax.axis_index(axis))
    pieces = jax.tree.map(lambda part: lax.all_gather(part, axis), value)
    subtotal = jax.tree.map(
        lambda part, zero: jnp.full_like(part, 0) + jnp.asarray(zero, part.dtype), value, neutral
    )

    def turn(position, subtotal):
        longer = join(subtotal, jax.tree.map(lambda part: part[position], pieces))
        return jax.tree.map(lambda new, old: jnp.where(position < mine, new, old), longer, subtotal)

    return lax.fori_loop(0, count - 1, turn, subtotal)


def passed_along(block, axis, distance):
    devices = range(lax.axis_size(axis))
    route = [(i - distance, i) for i in devices if i - distance in devices]
    return lax.ppermute(block, axis, route)


def taylor_tree(extended, stride, margin):
    length = extended.shape[-1]
    current = extended[:, None, :]
    blocks_width = 1
    while current.shape[0] > 1:
        former = current[0::2]
        latter = jnp.pad(current[1::2], ((0, 0), (0, 0), (0, margin)))
        merged = []
        for half_idx in range(blocks_width):
            anchor = former[:, half_idx]
            source = latter[:, half_idx]
            merged.append(
                anchor + lax.dynamic_slice_in_dim(source, half_idx * stride, length, axis=1)
            )
            merged.append(
                anchor + lax.dynamic_slice_in_dim(source, (half_idx + 1) * stride, length, axis=1)
            )
        current = jnp.stack(merged, axis=1)
        blocks_width = blocks_width * 2
    return current[0]


def score_rate(extended, stride, cut_row, chan_dev, margin):
    drifts = taylor_tree(extended, stride, margin)[:, :chan_dev]
    cut_levels = cut_row.astype(jnp.float32) / 256.0
    return jnp.mean(jax.nn.relu(0.25 * drifts - cut_levels[:, None]), axis=0)


def block_layout(chan_dev):
    width = min(1024, chan_dev)
    return (width, chan_dev // width)


def bin_partials(summed, bandpass_bin, total_bins, integrations):
    group_dev, chan_dev = summed.shape
    width, blocks = block_layout(chan_dev)
    bins_iota = jnp.arange(total_bins, dtype=jnp.int32)
    values = jnp.transpose(summed.reshape(group_dev, blocks, width), (1, 0, 2))
    indices = bandpass_bin.reshape(blocks, width)

    def bin_one_block(carry, items):
        block_values, block_index = items
        one_hot = (block_index[:, None] == bins_iota[None, :]).astype(jnp.float32)
        sums = carry[0] + jnp.dot(
            block_values,
            one_hot,
            precision=lax.Precision.HIGHEST,
            preferred_element_type=jnp.float32,
        )
        counts = carry[1] + jnp.sum(one_hot, axis=0)
        return ((sums, counts), None)

    start = (jnp.zeros((group_dev, total_bins), jnp.float32), jnp.zeros((total_bins,), jnp.float32))
    (bin_sums, counts), unused = lax.scan(bin_one_block, start, (values, indices))
    tallies = jnp.broadcast_to(float(integrations) * counts[None, :], bin_sums.shape)
    return (bin_sums, tallies)


def read_levels(running, bandpass_bin):
    group_dev, total_bins = running.shape
    chan_dev = bandpass_bin.shape[0]
    width, blocks = block_layout(chan_dev)
    bins_iota = jnp.arange(total_bins, dtype=jnp.int32)

    def read_one_block(carry, block_index):
        one_hot = (block_index[:, None] == bins_iota[None, :]).astype(jnp.float32)
        picked = lax.dot_general(
            running,
            one_hot,
            (((1,), (1,)), ((), ())),
            precision=lax.Precision.HIGHEST,
            preferred_element_type=jnp.float32,
        )
        return (carry, picked)

    unused, picked_blocks = lax.scan(read_one_block, 0, bandpass_bin.reshape(blocks, width))
    return jnp.transpose(picked_blocks, (1, 0, 2)).reshape(group_dev, chan_dev)


def add_pair(earlier, later):
    return (earlier[0] + later[0], earlier[1] + later[1])


def shards(spectra, channel_gain, bandpass_bin, drift_range, hit_cutoff):
    group_dev, integrations, chan_dev = spectra.shape
    total_bins = 4 * lax.axis_size("freq")
    calibrated = spectra * channel_gain[None, None, :]
    summed = jnp.sum(calibrated, axis=1)
    bin_sums, tallies = bin_partials(summed, bandpass_bin, total_bins, integrations)
    freq_sums, freq_tallies = lax.psum((bin_sums, tallies), "freq")
    zero_row = jnp.zeros((total_bins,), jnp.float32)
    before_sums, before_tallies = carried_in(
        (jnp.sum(freq_sums, axis=0), jnp.sum(freq_tallies, axis=0)),
        "section",
        add_pair,
        (zero_row, zero_row),
    )
    running = (before_sums[None, :] + jnp.cumsum(freq_sums, axis=0)) / (
        before_tallies[None, :] + jnp.cumsum(freq_tallies, axis=0)
    )
    levels = read_levels(running, bandpass_bin)
    normal = calibrated / levels[:, None, :] - 1.0
    rate_count = hit_cutoff.shape[1]
    margin = rate_count * (integrations - 1)
    right_rim = passed_along(normal[:, :, :margin], "freq", -1)
    section_first = lax.axis_index("section") * group_dev

    def one_group(position, scores):
        extended = jnp.concatenate([normal[position], right_rim[position]], axis=1)
        group_id = section_first + position
        for stride in range(1, rate_count + 1):
            result_row = lax.cond(
                stride <= drift_range[group_id],
                lambda: score_rate(
                    extended, stride, hit_cutoff[group_id, stride - 1], chan_dev, margin
                ),
                lambda: jnp.zeros((chan_dev,), jnp.float32),
            )
            scores = scores.at[position, stride - 1].set(result_row)
        return scores

    own_scores = lax.fori_loop(
        0, group_dev, one_group, jnp.zeros((group_dev, rate_count, chan_dev), jnp.float32)
    )
    return lax.all_to_all(own_scores, "section", split_axis=1, concat_axis=0, tiled=True)


def solution(mesh):
    return jax.shard_map(
        shards,
        mesh=mesh,
        in_specs=(P("section", None, "freq"), P("freq"), P("freq"), P(), P()),
        out_specs=P(None, "section", "freq"),
        check_vma=False,
    )
```

profile of v0, /device:TPU:0, one launch (start us, length us, event | category | flops | bytes accessed | tf_op | source)
XLA Modules:
  0.0 124.3 jit_solution(13200664469159023011)
XLA Ops:
  0.0 0.8 reshape.207
  0.8 1.6 %multiply_reduce_fusion = f32[2,8192]{1,0:T(2,128)S(1)} fusion(f32[2,16,8192]{2,1,0:T(8,128)} %param.19, f32[8192]{0:T(1024)S(1)} %copy-done.1), kind=kLoop, calls=%fused_computation.218 | loop fusion | flops 507904 | bytes 1146880 | tf_op jit(solution)/shard_map/reduce_sum | solution.py:114
  2.4 3.4 %while.47 = (s32[]{:T(128)}, f32[2,64]{1,0:T(2,128)S(1)}, f32[64]{0:T(128)S(1)}, f32[8,2,1024]{2,1,0:T(2,128)S(1)}, s32[8,1024]{1,0:T(8,128)S(1)}, /*index=5*/s32[]{:T(128)}, s32[]{:T(128)}) while((s32[]{:T(128)}, f32[2,64]{1,0:T(2,128)S(1)}, f32[64]{0:T(128)S(1)}, f32[8,2,1024]{2,1,0:T(2,128)S(1)}, s32[8,1024]{1,0:T(8,128)S(1)}, ...), condition=%wide.region_3.4_spmd.clone, body=%wide.region_1.3_spmd.clone.sunk | while | flops 1835331 | bytes 27232 | solution.py:80
  5.8 34.9 %all-reduce.10 = (f32[2,64]{1,0:T(2,128)S(1)}, f32[2,64]{1,0:T(2,128)S(1)}) all-reduce(f32[2,64]{1,0:T(2,128)S(1)} %broadcast_in_dim.43, f32[2,64]{1,0:T(2,128)S(1)} %get-tuple-element.288), channel_id=1, replica_groups=mesh['section'=2,'freq'=16] {'freq'}, use_global_device_ids=true, to_apply=%region_7.8 | all-reduce | flops 256 | bytes 2048 | tf_op jit(solution)/shard_map/psum | solution.py:116
  40.8 0.6 copy-done.4
  41.4 0.6 dynamic-slice.38
  43.1 4.9 %all-reduce.11 = (f32[128]{0:T(128)S(1)}, f32[128]{0:T(128)S(1)}) all-reduce(f32[128]{0:T(128)S(1)} %dynamic-update-slice.15, f32[128]{0:T(128)S(1)} %dynamic-update-slice.14), channel_id=3, replica_groups=mesh['section'=2,'freq'=16] {'section'}, use_global_device_ids=true, to_apply=%add.9 | all-reduce | flops 256 | bytes 2048
  48.1 3.8 %while.46 = (s32[]{:T(128)}, f32[8,2,1024]{2,1,0:T(2,128)S(1)}, s32[8,1024]{1,0:T(8,128)S(1)}, f32[2,64]{1,0:T(2,128)S(1)}, s32[]{:T(128)}) while((s32[]{:T(128)}, f32[8,2,1024]{2,1,0:T(2,128)S(1)}, s32[8,1024]{1,0:T(8,128)S(1)}, f32[2,64]{1,0:T(2,128)S(1)}, s32[]{:T(128)}) %tuple.198), condition=%wide.region_11.12_spmd.clone, body=%wide.region_10.11_spmd.clone.sunk | while | flops 1638402 | bytes 21573 | solution.py:102
  52.1 1.3 %collective-permute-start = (f32[2,16,30]{2,1,0:T(8,128)S(1)}, f32[2,16,30]{2,1,0:T(8,128)S(1)}, u32[]{:S(2)}, u32[]{:S(2)}) collective-permute-start(f32[2,16,30]{2,1,0:T(8,128)S(1)} %slice.378), channel_id=1, source_target_pairs={{1,0},{2,1},{3,2},{4,3},{5,4},{6,5},{7,6},{8,7},{9,8},{10,9},{11,1... | collective-permute-start | bytes 11528 | tf_op jit(solution)/shard_map/ppermute | solution.py:24
  53.4 1.8 %collective-permute-done = f32[2,16,30]{2,1,0:T(8,128)S(1)} collective-permute-done((f32[2,16,30]{2,1,0:T(8,128)S(1)}, f32[2,16,30]{2,1,0:T(8,128)S(1)}, u32[]{:S(2)}, u32[]{:S(2)}) %collective-permute-start) | collective-permute-done | bytes 3872 | tf_op jit(solution)/shard_map/ppermute | solution.py:24
  55.2 61.3 %while.45 = (s32[]{:T(128)}, f32[2,2,8192]{2,1,0:T(2,128)S(1)}, s32[]{:T(128)}, s32[4]{0:T(128)S(1)}, f32[2,16,8192]{2,1,0:T(8,128)S(1)}, /*index=5*/f32[2,16,30...) while((s32[]{:T(128)}, f32[2,2,8192]{2,1,0:T(2,128)S(1)}, ...), condition=%wide.region_21.22_spmd, body=%wide.region_12.21_spmd.sunk | while | flops 3301456 | bytes 33727040 | solution.py:148
  55.2 0.6 dynamic_slice.474
  56.6 17.2 %conditional.4 = (f32[1,1,8192]{2,1,0:T(1,128)S(1)}) conditional(s32[]{:T(128)} %bitcast.327, () %tuple.180, (f32[16,8222]{1,0:T(8,128)S(1)}, s32[]{:T(128)}, s32[4,2,16]{2,1,0:T(2,128)}) %tuple.181), branch_computations={%region_14.14_spmd, %region_15.16_spmd} | conditional | flops 1576738 | bytes 15647118 | solution.py:138
  56.6 0.9 slice.271
  57.6 0.9 slice.270
  58.8 1.7 %slice.274 = f32[4,2,8222]{2,0,1:T(4,128)S(1)} slice(f32[8,2,8222]{2,0,1:T(8,128)S(1)} %pad_maximum_fusion), slice={[1:8:2], [0:2:1], [0:8222:1]} | slice | bytes 526208 | tf_op jit(solution)/shard_map/while/body/eval_jaxpr/cond/branch_1_fun/slice | solution.py:33
  60.5 1.7 %slice.272 = f32[4,2,8222]{2,0,1:T(4,128)S(1)} slice(f32[8,2,8222]{2,0,1:T(8,128)S(1)} %pad_maximum_fusion), slice={[0:8:2], [0:2:1], [0:8222:1]} | slice | bytes 526208 | tf_op jit(solution)/shard_map/while/body/eval_jaxpr/cond/branch_1_fun/slice | solution.py:32
  62.5 2.2 %slice.280 = f32[2,4,8222]{2,0,1:T(2,128)S(1)} slice(f32[4,4,8222]{2,0,1:T(4,128)S(1)} %pad_maximum_fusion.1), slice={[1:4:2], [0:4:1], [0:8222:1]} | slice | bytes 526208 | tf_op jit(solution)/shard_map/while/body/eval_jaxpr/cond/branch_1_fun/slice | solution.py:33
  64.8 2.2 %slice.278 = f32[2,4,8222]{2,0,1:T(2,128)S(1)} slice(f32[4,4,8222]{2,0,1:T(4,128)S(1)} %pad_maximum_fusion.1), slice={[0:4:2], [0:4:1], [0:8222:1]} | slice | bytes 526208 | tf_op jit(solution)/shard_map/while/body/eval_jaxpr/cond/branch_1_fun/slice | solution.py:32
  69.8 3.0 %stack.169 = f32[1,16,8222]{2,1,0:T(8,128)S(1)} concatenate(f32[1,1,8222]{2,1,0:T(1,128)S(1)} %get-tuple-element.436, f32[1,1,8222]{2,1,0:T(1,128)S(1)} %get-tuple-element.437, f32[1,1,8222]{2,1,0:T(1,128)S(1)} %get-tuple-element.427, f32[1,1,8222]{2,1,0:T(1,128)S(1)} %get-tuple-element.426, f32[1,1,8222]{2,1,0:T(1,128)S(1)} %get-tuple-element.434, ...), dimensions={1} | concatenate | bytes 1052416 | tf_op jit(solution)/shard_map/while/body/eval_jaxpr/cond/branch_1_fun/stack | solution.py:44
  72.9 0.7 multiply_bitcast_fusion
  73.8 0.8 and_reduce_fusion.3
  74.6 0.7 broadcast_select_fusion.7
  76.3 0.6 broadcast_select_fusion.8
  77.3 0.6 dynamic_slice.474
  78.7 17.2 %conditional.4 = (f32[1,1,8192]{2,1,0:T(1,128)S(1)}) conditional(s32[]{:T(128)} %bitcast.327, () %tuple.180, (f32[16,8222]{1,0:T(8,128)S(1)}, s32[]{:T(128)}, s32[4,2,16]{2,1,0:T(2,128)}) %tuple.181), branch_computations={%region_14.14_spmd, %region_15.16_spmd} | conditional | flops 1576738 | bytes 15647118 | solution.py:138
  78.7 0.9 slice.271
  79.7 0.9 slice.270
  80.8 1.7 %slice.274 = f32[4,2,8222]{2,0,1:T(4,128)S(1)} slice(f32[8,2,8222]{2,0,1:T(8,128)S(1)} %pad_maximum_fusion), slice={[1:8:2], [0:2:1], [0:8222:1]} | slice | bytes 526208 | tf_op jit(solution)/shard_map/while/body/eval_jaxpr/cond/branch_1_fun/slice | solution.py:33
  82.5 1.7 %slice.272 = f32[4,2,8222]{2,0,1:T(4,128)S(1)} slice(f32[8,2,8222]{2,0,1:T(8,128)S(1)} %pad_maximum_fusion), slice={[0:8:2], [0:2:1], [0:8222:1]} | slice | bytes 526208 | tf_op jit(solution)/shard_map/while/body/eval_jaxpr/cond/branch_1_fun/slice | solution.py:32
  84.6 2.2 %slice.280 = f32[2,4,8222]{2,0,1:T(2,128)S(1)} slice(f32[4,4,8222]{2,0,1:T(4,128)S(1)} %pad_maximum_fusion.1), slice={[1:4:2], [0:4:1], [0:8222:1]} | slice | bytes 526208 | tf_op jit(solution)/shard_map/while/body/eval_jaxpr/cond/branch_1_fun/slice | solution.py:33
  86.8 2.2 %slice.278 = f32[2,4,8222]{2,0,1:T(2,128)S(1)} slice(f32[4,4,8222]{2,0,1:T(4,128)S(1)} %pad_maximum_fusion.1), slice={[0:4:2], [0:4:1], [0:8222:1]} | slice | bytes 526208 | tf_op jit(solution)/shard_map/while/body/eval_jaxpr/cond/branch_1_fun/slice | solution.py:32
  91.9 3.0 %stack.169 = f32[1,16,8222]{2,1,0:T(8,128)S(1)} concatenate(f32[1,1,8222]{2,1,0:T(1,128)S(1)} %get-tuple-element.436, f32[1,1,8222]{2,1,0:T(1,128)S(1)} %get-tuple-element.437, f32[1,1,8222]{2,1,0:T(1,128)S(1)} %get-tuple-element.427, f32[1,1,8222]{2,1,0:T(1,128)S(1)} %get-tuple-element.426, f32[1,1,8222]{2,1,0:T(1,128)S(1)} %get-tuple-element.434, ...), dimensions={1} | concatenate | bytes 1052416 | tf_op jit(solution)/shard_map/while/body/eval_jaxpr/cond/branch_1_fun/stack | solution.py:44
  94.9 0.7 multiply_bitcast_fusion
  95.8 0.8 and_reduce_fusion.3
  96.6 0.7 broadcast_select_fusion.7
  98.3 17.2 %conditional.5 = (f32[1,1,8192]{2,1,0:T(1,128)S(1)}) conditional(s32[]{:T(128)} %bitcast.329, () %tuple.182, (f32[16,8222]{1,0:T(8,128)S(1)}, s32[]{:T(128)}, s32[4,2,16]{2,1,0:T(2,128)}) %tuple.181), branch_computations={%region_18.18_spmd, %region_19.20_spmd} | conditional | flops 1576738 | bytes 15647118 | solution.py:138
  98.4 0.9 slice.307
  99.3 0.9 slice.306
  100.5 1.7 %slice.310 = f32[4,2,8222]{2,0,1:T(4,128)S(1)} slice(f32[8,2,8222]{2,0,1:T(8,128)S(1)} %pad_maximum_fusion.2), slice={[1:8:2], [0:2:1], [0:8222:1]} | slice | bytes 526208 | tf_op jit(solution)/shard_map/while/body/eval_jaxpr/cond/branch_1_fun/slice | solution.py:33
  102.2 1.7 %slice.308 = f32[4,2,8222]{2,0,1:T(4,128)S(1)} slice(f32[8,2,8222]{2,0,1:T(8,128)S(1)} %pad_maximum_fusion.2), slice={[0:8:2], [0:2:1], [0:8222:1]} | slice | bytes 526208 | tf_op jit(solution)/shard_map/while/body/eval_jaxpr/cond/branch_1_fun/slice | solution.py:32
  104.3 2.2 %slice.316 = f32[2,4,8222]{2,0,1:T(2,128)S(1)} slice(f32[4,4,8222]{2,0,1:T(4,128)S(1)} %pad_maximum_fusion.3), slice={[1:4:2], [0:4:1], [0:8222:1]} | slice | bytes 526208 | tf_op jit(solution)/shard_map/while/body/eval_jaxpr/cond/branch_1_fun/slice | solution.py:33
  106.5 2.2 %slice.314 = f32[2,4,8222]{2,0,1:T(2,128)S(1)} slice(f32[4,4,8222]{2,0,1:T(4,128)S(1)} %pad_maximum_fusion.3), slice={[0:4:2], [0:4:1], [0:8222:1]} | slice | bytes 526208 | tf_op jit(solution)/shard_map/while/body/eval_jaxpr/cond/branch_1_fun/slice | solution.py:32
  111.6 3.0 %stack.203 = f32[1,16,8222]{2,1,0:T(8,128)S(1)} concatenate(f32[1,1,8222]{2,1,0:T(1,128)S(1)} %get-tuple-element.482, f32[1,1,8222]{2,1,0:T(1,128)S(1)} %get-tuple-element.483, f32[1,1,8222]{2,1,0:T(1,128)S(1)} %get-tuple-element.473, f32[1,1,8222]{2,1,0:T(1,128)S(1)} %get-tuple-element.472, f32[1,1,8222]{2,1,0:T(1,128)S(1)} %get-tuple-element.480, ...), dimensions={1} | concatenate | bytes 1052416 | tf_op jit(solution)/shard_map/while/body/eval_jaxpr/cond/branch_1_fun/stack | solution.py:44
  114.6 0.7 multiply_bitcast_fusion.1
  115.5 0.6 broadcast_select_fusion.8
  116.6 6.8 %all_to_all.19 = f32[2,2,8192]{2,0,1:T(2,128)S(1)} all-to-all(f32[2,2,8192]{2,0,1:T(2,128)S(1)} %copy.9), channel_id=1, replica_groups=mesh['section'=2,'freq'=16] {'section'}, dimensions={1} | all-to-all | bytes 262144 | tf_op jit(solution)/shard_map/all_to_all | solution.py:151
  123.4 0.9 all_to_all.17
  (157 shorter events, 20.3 us)
Async XLA Ops:
  0.0 0.8 copy-start.1
  0.8 51.1 %copy-start = (f32[2,16,8192]{2,1,0:T(8,128)S(1)}, f32[2,16,8192]{2,1,0:T(8,128)}, u32[]{:S(2)}) copy-start(f32[2,16,8192]{2,1,0:T(8,128)} %param.19) | copy-start | bytes 3145732
  40.8 0.7 copy-start.4
  52.1 3.1 %collective-permute-start = (f32[2,16,30]{2,1,0:T(8,128)S(1)}, f32[2,16,30]{2,1,0:T(8,128)S(1)}, u32[]{:S(2)}, u32[]{:S(2)}) collective-permute-start(f32[2,16,30]{2,1,0:T(8,128)S(1)} %slice.378), channel_id=1, source_target_pairs={{1,0},{2,1},{3,2},{4,3},{5,4},{6,5},{7,6},{8,7},{9,8},{10,9},{11,1... | collective-permute-start | bytes 11528 | tf_op jit(solution)/shard_map/ppermute | solution.py:24
  53.4 1.8 %copy-start.2 = (s32[3]{0:T(128)S(1)}, s32[3]{0:T(128)}, u32[]{:S(2)}) copy-start(s32[3]{0:T(128)} %constant.199.clone.1) | copy-start | bytes 40
  53.4 1.8 %copy-start.3 = (s32[4]{0:T(128)S(1)}, s32[4]{0:T(128)}, u32[]{:S(2)}) copy-start(s32[4]{0:T(128)} %param.22) | copy-start | bytes 52
where the time goes:
time: 125 us; the launch traced here: 124 us
  blocking collectives  46.7 us (37%)
  local copies, waits for them, and re-layouts  45.2 us (36%)
  other arithmetic  19.7 us (16%)
  matrix products  5.12 us (4%)
  loops' own time  3.79 us (3%)
  waiting for transfers between devices  1.75 us (1%)
  starting transfers between devices  1.29 us (1%)
    psum x1, blocking collectives, shards(): freq_sums, freq_tallies = lax.psum((bin_sums, tallies), 'freq')  34.9 us
    slice x12, local copies, waits for them, and re-layouts, taylor_tree(): latter = jnp.pad(current[1::2], ((0, 0), (0, 0), (0, margin)))  15.2 us
    slice x9, local copies, waits for them, and re-layouts, taylor_tree(): former = current[0::2]  14.4 us
    another operation x3, local copies, waits for them, and re-layouts, taylor_tree(): current = jnp.stack(merged, axis=1)  9.09 us
    all_to_all x1, blocking collectives, shards(): lax.all_to_all(own_scores, 'section', split_axis=1, concat_axis=0, tiled=...  6.85 us
    another operation x27, other arithmetic, taylor_tree(): current = jnp.stack(merged, axis=1)  6.26 us
    unnamed x1, blocking collectives  4.91 us
    another operation x6, other arithmetic  4.22 us
  transfers between devices with their start and end apart: 1, of which 1 were waited for; matrix products, arithmetic and copies ran while one was open for 0% of the time, Pallas kernels for 0%

commit v1 on v0

--- a/solution.py
+++ b/solution.py
@@ -148,7 +148,12 @@
     own_scores = lax.fori_loop(
         0, group_dev, one_group, jnp.zeros((group_dev, rate_count, chan_dev), jnp.float32)
     )
-    return lax.all_to_all(own_scores, "section", split_axis=1, concat_axis=0, tiled=True)
+    return jnp.concatenate(
+        lax.all_to_all(
+            jnp.stack(jnp.split(own_scores, lax.axis_size("section"), axis=1)), "section", 0, 0
+        ),
+        axis=0,
+    )
 
 
 def solution(mesh):

time: 125 us -> 125 us (level)
    another operation x6 -> x7, other arithmetic: 4.22 us -> 4.63 us
where the time goes in v1:
time: 125 us; the launch traced here: 124 us
  blocking collectives  46.7 us (37%)
  local copies, waits for them, and re-layouts  44.9 us (36%)
  other arithmetic  20.1 us (16%)
  matrix products  5.12 us (4%)
  loops' own time  3.43 us (3%)
  waiting for transfers between devices  1.75 us (1%)
  starting transfers between devices  1.29 us (1%)
    psum x1, blocking collectives, shards(): freq_sums, freq_tallies = lax.psum((bin_sums, tallies), 'freq')  34.9 us
    slice x12, local copies, waits for them, and re-layouts, taylor_tree(): latter = jnp.pad(current[1::2], ((0, 0), (0, 0), (0, margin)))  15.2 us
    slice x9, local copies, waits for them, and re-layouts, taylor_tree(): former = current[0::2]  14.4 us
    another operation x3, local copies, waits for them, and re-layouts, taylor_tree(): current = jnp.stack(merged, axis=1)  9.09 us
    all_to_all x1, blocking collectives, shards(): lax.all_to_all(jnp.stack(jnp.split(own_scores, lax.axis_size('section'),...  6.85 us
    another operation x27, other arithmetic, taylor_tree(): current = jnp.stack(merged, axis=1)  6.26 us
    unnamed x1, blocking collectives  4.91 us
    another operation x6, other arithmetic  4.51 us
  transfers between devices with their start and end apart: 1, of which 1 were waited for; matrix products, arithmetic and copies ran while one was open for 0% of the time, Pallas kernels for 0%

profile of v1, /device:TPU:0, one launch (start us, length us, event | category | flops | bytes accessed | tf_op | source)
XLA Modules:
  0.0 124.1 jit_solution(5124658437611934114)
XLA Ops:
  0.0 0.8 reshape.210
  0.8 1.6 %multiply_reduce_fusion = f32[2,8192]{1,0:T(2,128)S(1)} fusion(f32[2,16,8192]{2,1,0:T(8,128)} %param.19, f32[8192]{0:T(1024)S(1)} %copy-done.1), kind=kLoop, calls=%fused_computation.218 | loop fusion | flops 507904 | bytes 1146880 | tf_op jit(solution)/shard_map/reduce_sum | solution.py:114
  2.4 3.4 %while.47 = (s32[]{:T(128)}, f32[2,64]{1,0:T(2,128)S(1)}, f32[64]{0:T(128)S(1)}, f32[8,2,1024]{2,1,0:T(2,128)S(1)}, s32[8,1024]{1,0:T(8,128)S(1)}, /*index=5*/s32[]{:T(128)}, s32[]{:T(128)}) while((s32[]{:T(128)}, f32[2,64]{1,0:T(2,128)S(1)}, f32[64]{0:T(128)S(1)}, f32[8,2,1024]{2,1,0:T(2,128)S(1)}, s32[8,1024]{1,0:T(8,128)S(1)}, ...), condition=%wide.region_3.4_spmd.clone, body=%wide.region_1.3_spmd.clone.sunk | while | flops 1835331 | bytes 27232 | solution.py:80
  5.8 34.9 %all-reduce.10 = (f32[2,64]{1,0:T(2,128)S(1)}, f32[2,64]{1,0:T(2,128)S(1)}) all-reduce(f32[2,64]{1,0:T(2,128)S(1)} %broadcast_in_dim.43, f32[2,64]{1,0:T(2,128)S(1)} %get-tuple-element.288), channel_id=1, replica_groups=mesh['section'=2,'freq'=16] {'freq'}, use_global_device_ids=true, to_apply=%region_7.8 | all-reduce | flops 256 | bytes 2048 | tf_op jit(solution)/shard_map/psum | solution.py:116
  40.8 0.6 copy-done.4
  41.4 0.6 dynamic-slice.38
  43.2 4.9 %all-reduce.11 = (f32[128]{0:T(128)S(1)}, f32[128]{0:T(128)S(1)}) all-reduce(f32[128]{0:T(128)S(1)} %dynamic-update-slice.15, f32[128]{0:T(128)S(1)} %dynamic-update-slice.14), channel_id=3, replica_groups=mesh['section'=2,'freq'=16] {'section'}, use_global_device_ids=true, to_apply=%add.9 | all-reduce | flops 256 | bytes 2048
  48.1 3.8 %while.46 = (s32[]{:T(128)}, f32[8,2,1024]{2,1,0:T(2,128)S(1)}, s32[8,1024]{1,0:T(8,128)S(1)}, f32[2,64]{1,0:T(2,128)S(1)}, s32[]{:T(128)}) while((s32[]{:T(128)}, f32[8,2,1024]{2,1,0:T(2,128)S(1)}, s32[8,1024]{1,0:T(8,128)S(1)}, f32[2,64]{1,0:T(2,128)S(1)}, s32[]{:T(128)}) %tuple.199), condition=%wide.region_11.12_spmd.clone, body=%wide.region_10.11_spmd.clone.sunk | while | flops 1638402 | bytes 21573 | solution.py:102
  52.1 1.3 %collective-permute-start = (f32[2,16,30]{2,1,0:T(8,128)S(1)}, f32[2,16,30]{2,1,0:T(8,128)S(1)}, u32[]{:S(2)}, u32[]{:S(2)}) collective-permute-start(f32[2,16,30]{2,1,0:T(8,128)S(1)} %slice.378), channel_id=1, source_target_pairs={{1,0},{2,1},{3,2},{4,3},{5,4},{6,5},{7,6},{8,7},{9,8},{10,9},{11,1... | collective-permute-start | bytes 11528 | tf_op jit(solution)/shard_map/ppermute | solution.py:24
  53.4 1.8 %collective-permute-done = f32[2,16,30]{2,1,0:T(8,128)S(1)} collective-permute-done((f32[2,16,30]{2,1,0:T(8,128)S(1)}, f32[2,16,30]{2,1,0:T(8,128)S(1)}, u32[]{:S(2)}, u32[]{:S(2)}) %collective-permute-start) | collective-permute-done | bytes 3872 | tf_op jit(solution)/shard_map/ppermute | solution.py:24
  55.2 61.1 %while.45 = (s32[]{:T(128)}, f32[2,2,8192]{2,1,0:T(2,128)S(1)}, s32[]{:T(128)}, s32[4]{0:T(128)S(1)}, f32[2,16,8192]{2,1,0:T(8,128)S(1)}, /*index=5*/f32[2,16,30...) while((s32[]{:T(128)}, f32[2,2,8192]{2,1,0:T(2,128)S(1)}, ...), condition=%wide.region_21.22_spmd, body=%wide.region_12.21_spmd.sunk | while | flops 3301456 | bytes 33727040 | solution.py:148
  55.2 0.6 dynamic_slice.474
  56.5 17.2 %conditional.4 = (f32[1,1,8192]{2,1,0:T(1,128)S(1)}) conditional(s32[]{:T(128)} %bitcast.327, () %tuple.181, (f32[16,8222]{1,0:T(8,128)S(1)}, s32[]{:T(128)}, s32[4,2,16]{2,1,0:T(2,128)}) %tuple.182), branch_computations={%region_14.14_spmd, %region_15.16_spmd} | conditional | flops 1576738 | bytes 15647118 | solution.py:138
  56.5 0.9 slice.271
  57.5 0.9 slice.270
  58.6 1.7 %slice.274 = f32[4,2,8222]{2,0,1:T(4,128)S(1)} slice(f32[8,2,8222]{2,0,1:T(8,128)S(1)} %pad_maximum_fusion), slice={[1:8:2], [0:2:1], [0:8222:1]} | slice | bytes 526208 | tf_op jit(solution)/shard_map/while/body/eval_jaxpr/cond/branch_1_fun/slice | solution.py:33
  60.3 1.7 %slice.272 = f32[4,2,8222]{2,0,1:T(4,128)S(1)} slice(f32[8,2,8222]{2,0,1:T(8,128)S(1)} %pad_maximum_fusion), slice={[0:8:2], [0:2:1], [0:8222:1]} | slice | bytes 526208 | tf_op jit(solution)/shard_map/while/body/eval_jaxpr/cond/branch_1_fun/slice | solution.py:32
  62.4 2.2 %slice.280 = f32[2,4,8222]{2,0,1:T(2,128)S(1)} slice(f32[4,4,8222]{2,0,1:T(4,128)S(1)} %pad_maximum_fusion.1), slice={[1:4:2], [0:4:1], [0:8222:1]} | slice | bytes 526208 | tf_op jit(solution)/shard_map/while/body/eval_jaxpr/cond/branch_1_fun/slice | solution.py:33
  64.6 2.2 %slice.278 = f32[2,4,8222]{2,0,1:T(2,128)S(1)} slice(f32[4,4,8222]{2,0,1:T(4,128)S(1)} %pad_maximum_fusion.1), slice={[0:4:2], [0:4:1], [0:8222:1]} | slice | bytes 526208 | tf_op jit(solution)/shard_map/while/body/eval_jaxpr/cond/branch_1_fun/slice | solution.py:32
  69.7 3.0 %stack.175 = f32[1,16,8222]{2,1,0:T(8,128)S(1)} concatenate(f32[1,1,8222]{2,1,0:T(1,128)S(1)} %get-tuple-element.436, f32[1,1,8222]{2,1,0:T(1,128)S(1)} %get-tuple-element.437, f32[1,1,8222]{2,1,0:T(1,128)S(1)} %get-tuple-element.427, f32[1,1,8222]{2,1,0:T(1,128)S(1)} %get-tuple-element.426, f32[1,1,8222]{2,1,0:T(1,128)S(1)} %get-tuple-element.434, ...), dimensions={1} | concatenate | bytes 1052416 | tf_op jit(solution)/shard_map/while/body/eval_jaxpr/cond/branch_1_fun/stack | solution.py:44
  72.8 0.7 multiply_bitcast_fusion
  73.7 0.8 and_reduce_fusion.3
  74.5 0.7 broadcast_select_fusion.7
  76.1 0.7 broadcast_select_fusion.8
  77.2 0.6 dynamic_slice.474
  78.4 17.2 %conditional.4 = (f32[1,1,8192]{2,1,0:T(1,128)S(1)}) conditional(s32[]{:T(128)} %bitcast.327, () %tuple.181, (f32[16,8222]{1,0:T(8,128)S(1)}, s32[]{:T(128)}, s32[4,2,16]{2,1,0:T(2,128)}) %tuple.182), branch_computations={%region_14.14_spmd, %region_15.16_spmd} | conditional | flops 1576738 | bytes 15647118 | solution.py:138
  78.5 0.9 slice.271
  79.4 0.9 slice.270
  80.6 1.7 %slice.274 = f32[4,2,8222]{2,0,1:T(4,128)S(1)} slice(f32[8,2,8222]{2,0,1:T(8,128)S(1)} %pad_maximum_fusion), slice={[1:8:2], [0:2:1], [0:8222:1]} | slice | bytes 526208 | tf_op jit(solution)/shard_map/while/body/eval_jaxpr/cond/branch_1_fun/slice | solution.py:33
  82.3 1.7 %slice.272 = f32[4,2,8222]{2,0,1:T(4,128)S(1)} slice(f32[8,2,8222]{2,0,1:T(8,128)S(1)} %pad_maximum_fusion), slice={[0:8:2], [0:2:1], [0:8222:1]} | slice | bytes 526208 | tf_op jit(solution)/shard_map/while/body/eval_jaxpr/cond/branch_1_fun/slice | solution.py:32
  84.4 2.2 %slice.280 = f32[2,4,8222]{2,0,1:T(2,128)S(1)} slice(f32[4,4,8222]{2,0,1:T(4,128)S(1)} %pad_maximum_fusion.1), slice={[1:4:2], [0:4:1], [0:8222:1]} | slice | bytes 526208 | tf_op jit(solution)/shard_map/while/body/eval_jaxpr/cond/branch_1_fun/slice | solution.py:33
  86.6 2.2 %slice.278 = f32[2,4,8222]{2,0,1:T(2,128)S(1)} slice(f32[4,4,8222]{2,0,1:T(4,128)S(1)} %pad_maximum_fusion.1), slice={[0:4:2], [0:4:1], [0:8222:1]} | slice | bytes 526208 | tf_op jit(solution)/shard_map/while/body/eval_jaxpr/cond/branch_1_fun/slice | solution.py:32
  91.7 3.0 %stack.175 = f32[1,16,8222]{2,1,0:T(8,128)S(1)} concatenate(f32[1,1,8222]{2,1,0:T(1,128)S(1)} %get-tuple-element.436, f32[1,1,8222]{2,1,0:T(1,128)S(1)} %get-tuple-element.437, f32[1,1,8222]{2,1,0:T(1,128)S(1)} %get-tuple-element.427, f32[1,1,8222]{2,1,0:T(1,128)S(1)} %get-tuple-element.426, f32[1,1,8222]{2,1,0:T(1,128)S(1)} %get-tuple-element.434, ...), dimensions={1} | concatenate | bytes 1052416 | tf_op jit(solution)/shard_map/while/body/eval_jaxpr/cond/branch_1_fun/stack | solution.py:44
  94.7 0.7 multiply_bitcast_fusion
  95.6 0.8 and_reduce_fusion.3
  96.4 0.7 broadcast_select_fusion.7
  98.0 17.2 %conditional.5 = (f32[1,1,8192]{2,1,0:T(1,128)S(1)}) conditional(s32[]{:T(128)} %bitcast.329, () %tuple.183, (f32[16,8222]{1,0:T(8,128)S(1)}, s32[]{:T(128)}, s32[4,2,16]{2,1,0:T(2,128)}) %tuple.182), branch_computations={%region_18.18_spmd, %region_19.20_spmd} | conditional | flops 1576738 | bytes 15647118 | solution.py:138
  98.1 0.9 slice.307
  99.0 0.9 slice.306
  100.2 1.7 %slice.310 = f32[4,2,8222]{2,0,1:T(4,128)S(1)} slice(f32[8,2,8222]{2,0,1:T(8,128)S(1)} %pad_maximum_fusion.2), slice={[1:8:2], [0:2:1], [0:8222:1]} | slice | bytes 526208 | tf_op jit(solution)/shard_map/while/body/eval_jaxpr/cond/branch_1_fun/slice | solution.py:33
  101.9 1.7 %slice.308 = f32[4,2,8222]{2,0,1:T(4,128)S(1)} slice(f32[8,2,8222]{2,0,1:T(8,128)S(1)} %pad_maximum_fusion.2), slice={[0:8:2], [0:2:1], [0:8222:1]} | slice | bytes 526208 | tf_op jit(solution)/shard_map/while/body/eval_jaxpr/cond/branch_1_fun/slice | solution.py:32
  104.0 2.2 %slice.316 = f32[2,4,8222]{2,0,1:T(2,128)S(1)} slice(f32[4,4,8222]{2,0,1:T(4,128)S(1)} %pad_maximum_fusion.3), slice={[1:4:2], [0:4:1], [0:8222:1]} | slice | bytes 526208 | tf_op jit(solution)/shard_map/while/body/eval_jaxpr/cond/branch_1_fun/slice | solution.py:33
  106.2 2.2 %slice.314 = f32[2,4,8222]{2,0,1:T(2,128)S(1)} slice(f32[4,4,8222]{2,0,1:T(4,128)S(1)} %pad_maximum_fusion.3), slice={[0:4:2], [0:4:1], [0:8222:1]} | slice | bytes 526208 | tf_op jit(solution)/shard_map/while/body/eval_jaxpr/cond/branch_1_fun/slice | solution.py:32
  111.3 3.0 %stack.209 = f32[1,16,8222]{2,1,0:T(8,128)S(1)} concatenate(f32[1,1,8222]{2,1,0:T(1,128)S(1)} %get-tuple-element.482, f32[1,1,8222]{2,1,0:T(1,128)S(1)} %get-tuple-element.483, f32[1,1,8222]{2,1,0:T(1,128)S(1)} %get-tuple-element.473, f32[1,1,8222]{2,1,0:T(1,128)S(1)} %get-tuple-element.472, f32[1,1,8222]{2,1,0:T(1,128)S(1)} %get-tuple-element.480, ...), dimensions={1} | concatenate | bytes 1052416 | tf_op jit(solution)/shard_map/while/body/eval_jaxpr/cond/branch_1_fun/stack | solution.py:44
  114.3 0.7 multiply_bitcast_fusion.1
  115.2 0.7 broadcast_select_fusion.8
  116.6 6.8 %all_to_all.5 = f32[2,2,1,8192]{3,2,1,0:T(1,128)S(1)} all-to-all(f32[2,2,1,8192]{3,2,1,0:T(1,128)S(1)} %pad_maximum_fusion.5), channel_id=1, replica_groups=mesh['section'=2,'freq'=16] {'section'}, dimensions={0} | all-to-all | bytes 262144 | tf_op jit(solution)/shard_map/all_to_all | solution.py:152
  123.4 0.7 copy.55
  (158 shorter events, 20.5 us)
Async XLA Ops:
  0.0 0.8 copy-start.1
  0.8 51.1 %copy-start = (f32[2,16,8192]{2,1,0:T(8,128)S(1)}, f32[2,16,8192]{2,1,0:T(8,128)}, u32[]{:S(2)}) copy-start(f32[2,16,8192]{2,1,0:T(8,128)} %param.19) | copy-start | bytes 3145732
  40.8 0.7 copy-start.4
  52.1 3.1 %collective-permute-start = (f32[2,16,30]{2,1,0:T(8,128)S(1)}, f32[2,16,30]{2,1,0:T(8,128)S(1)}, u32[]{:S(2)}, u32[]{:S(2)}) collective-permute-start(f32[2,16,30]{2,1,0:T(8,128)S(1)} %slice.378), channel_id=1, source_target_pairs={{1,0},{2,1},{3,2},{4,3},{5,4},{6,5},{7,6},{8,7},{9,8},{10,9},{11,1... | collective-permute-start | bytes 11528 | tf_op jit(solution)/shard_map/ppermute | solution.py:24
  53.4 1.8 %copy-start.2 = (s32[3]{0:T(128)S(1)}, s32[3]{0:T(128)}, u32[]{:S(2)}) copy-start(s32[3]{0:T(128)} %constant.199.clone.1) | copy-start | bytes 40
  53.4 1.8 %copy-start.3 = (s32[4]{0:T(128)S(1)}, s32[4]{0:T(128)}, u32[]{:S(2)}) copy-start(s32[4]{0:T(128)} %param.22) | copy-start | bytes 52
